TPU v7x, 128 devices: a whole 4x4x4 slice. The times are simulated.
128 devices in a mesh: owner: 4 (over y_lo, core), rows: 32 (over z, y_hi, x).
Axes of the slice: x: 4, y: 4 (y_hi: 2, y_lo: 2; y = y_hi * 2 + y_lo), z: 4, core: 2. Of those that a mesh axis runs over, the one named last changes fastest.
Arguments:
- w_gate: float32 [64, 2048, 1024], P('owner', 'rows'), may hold values from -0.25 to 0.25
- avg_gate: float32 [64, 2048, 1024], P('owner', 'rows'), may hold values from -0.125 to 0.125
- w_up: float32 [64, 2048, 1024], P('owner', 'rows'), may hold values from -0.25 to 0.25
- avg_up: float32 [64, 2048, 1024], P('owner', 'rows'), may hold values from -0.125 to 0.125
- mix_share: float32 [64], P('owner'), may hold values from 0.2 to 0.8
- router_weight: float32 [2048, 64], P('rows', 'owner'), may hold values from -0.125 to 0.125
- router_gain: float32 [2048], P('rows'), may hold values from 0.25 to 1.75
Outputs:
- serve_gate: bfloat16 [64, 2048, 1024], P('owner', None, 'rows')
- serve_up: bfloat16 [64, 2048, 1024], P('owner', None, 'rows')
- scale_gate: float32 [64, 1024], P('owner', 'rows')
- scale_up: float32 [64, 1024], P('owner', 'rows')
- serve_router: bfloat16 [2048, 64], replicated
All inputs are finite; a program needn't handle non-finite values.
Results may differ from a plain program's by a relative error of at most 0.001.
Values may be sent and summed in bfloat16 or wider, within the bound.
A program may use at most 128 MiB of HBM per device.

v0:
```python
import jax
import jax.numpy as jnp
from jax import lax
from jax.sharding import PartitionSpec as P


def cut_along(shard, dim, devices):
    before, after = (shard.shape[:dim], shard.shape[dim + 1 :])
    return jnp.moveaxis(shard.reshape(*before, devices, -1, *after), dim, 0)


def summed_on_arrival(shard, axis, dim):
    devices = lax.axis_size(axis)
    tiles = lax.all_to_all(cut_along(shard, dim, devices), axis, 0, 0, tiled=True)
    return jnp.sum(tiles, axis=0)


def padded_to(lines, devices):
    spare = -len(lines) % devices
    return jnp.pad(lines, [(0, spare)] + [(0, 0)] * (lines.ndim - 1))


def laid_out(tiles, dim):
    dims = list(tiles.shape[1:])
    dims[dim] *= tiles.shape[0]
    return jnp.moveaxis(tiles, 0, dim).reshape(dims)


def copy_for_each(shard, axis):
    devices = lax.axis_size(axis)
    return lax.all_to_all(
        jnp.broadcast_to(shard[None], (devices, *shard.shape)), axis, 0, 0, tiled=True
    )


def gathered_copies(shard, axis, dim):
    return laid_out(copy_for_each(shard, axis), dim)


def nested_sum(shard, axes):
    own = summed_on_arrival(padded_to(shard, lax.axis_size(axes)), axes, 0)
    whole = gathered_copies(own, axes, 0)
    return whole[: len(shard)].reshape(shard.shape)


def together(arrays, axis):
    ends = [0]
    for a in arrays:
        ends.append(ends[-1] + a.size)
    running = nested_sum(jnp.concatenate([a.ravel() for a in arrays]), axis)
    return tuple((running[b:e].reshape(a.shape) for a, b, e in zip(arrays, ends, ends[1:])))


def body(w_gate, avg_gate, w_up, avg_up, mix_share, router_weight, router_gain):
    fresh_gate = mix_share[:, None, None] * w_gate + (1.0 - mix_share[:, None, None]) * avg_gate
    fresh_up = mix_share[:, None, None] * w_up + (1.0 - mix_share[:, None, None]) * avg_up
    total_gate, total_up = together(
        (jnp.sum(fresh_gate * fresh_gate, axis=1), jnp.sum(fresh_up * fresh_up, axis=1)), "rows"
    )
    scale_gate = jnp.sqrt(total_gate)
    scale_up = jnp.sqrt(total_up)
    narrow_gate, narrow_up = (
        (fresh_gate / jnp.expand_dims(scale_gate, 1)).astype(jnp.bfloat16),
        (fresh_up / jnp.expand_dims(scale_up, 1)).astype(jnp.bfloat16),
    )
    serve_gate, serve_up = (
        lax.all_to_all(narrow_gate, "rows", split_axis=2, concat_axis=1, tiled=True),
        lax.all_to_all(narrow_up, "rows", split_axis=2, concat_axis=1, tiled=True),
    )
    scale_gate = lax.dynamic_slice_in_dim(
        scale_gate, lax.axis_index("rows") * serve_gate.shape[2], serve_gate.shape[2], axis=1
    )
    scale_up = lax.dynamic_slice_in_dim(
        scale_up, lax.axis_index("rows") * serve_up.shape[2], serve_up.shape[2], axis=1
    )
    part_router = (router_weight * router_gain[:, None]).astype(jnp.bfloat16)
    row_router = gathered_copies(part_router, "rows", 0)
    serve_router = gathered_copies(row_router, "owner", 1)
    return (serve_gate, serve_up, scale_gate, scale_up, serve_router)


def solution(mesh):
    in_specs = (
        P("owner", "rows", None),
        P("owner", "rows", None),
        P("owner", "rows", None),
        P("owner", "rows", None),
        P("owner"),
        P("rows", "owner"),
        P("rows"),
    )
    out_specs = (
        P("owner", None, "rows"),
        P("owner", None, "rows"),
        P("owner", "rows"),
        P("owner", "rows"),
        P(),
    )
    return jax.shard_map(body, mesh=mesh, in_specs=in_specs, out_specs=out_specs, check_vma=False)
```

profile of v0, /device:TPU:0, one launch (start us, length us, event | category | flops | bytes accessed | tf_op | source)
XLA Modules:
  0.0 179.5 jit_solution(9206629035830946229)
XLA Ops:
  0.6 0.7 broadcast_subtract_fusion
  1.3 8.4 %multiply_reduce_fusion.1 = (f32[16,1024]{1,0:T(8,128)S(1)}, f32[16,1024]{1,0:T(8,128)S(1)}) fusion(f32[16,64,1024]{2,1,0:T(8,128)} %param.8, f32[16]{0:T(128)S(1)} %broadcast_subtract_fusion, f32[16,64,1024]{2,1,0:T(8,128)} %param.7, f32[16]{0:T(128)} %param.11, f32[16,64,1024]{2,1,0:T(8,128)} %param.10, f32[16,64,1024]{2,1,0:T(8,128)} %param.9), kind=kLoop, calls=%fused_computation.4 | loop fusion | flops 10452992 | bytes 16908416 | tf_op jit(solution)/shard_map/reduce_sum | solution.py:58
  9.7 0.7 all_to_all.42
  10.5 10.9 %all-to-all-start = ((f32[32,1,1024]{2,1,0:T(1,128)}), f32[32,1,1024]{2,1,0:T(1,128)S(1)}, u32[]{:S(2)}, u32[]{:S(2)}) async-start(f32[32,1,1024]{2,1,0:T(1,128)} %all_to_all.42), calls=%async_computation | async-start | bytes 262144 | tf_op jit(solution)/shard_map/all_to_all | solution.py:14
  21.5 0.8 reshape.56
  22.2 9.4 %all-to-all-done = f32[32,1,1024]{2,1,0:T(1,128)S(1)} async-done(((f32[32,1,1024]{2,1,0:T(1,128)}), f32[32,1,1024]{2,1,0:T(1,128)S(1)}, u32[]{:S(2)}, u32[]{:S(2)}) %all-to-all-start) | async-done | bytes 131104 | tf_op jit(solution)/shard_map/all_to_all | solution.py:14
  31.7 3.9 %all-to-all-start.4 = ((bf16[32,2,512]{2,1,0:T(2,128)(2,1)}), bf16[32,2,512]{2,1,0:T(2,128)(2,1)S(1)}, u32[]{:S(2)}, u32[]{:S(2)}) async-start(bf16[32,2,512]{2,1,0:T(2,128)(2,1)} %reshape.56), calls=%async_computation.4 | async-start | bytes 131072 | tf_op jit(solution)/shard_map/all_to_all | solution.py:31
  35.6 9.9 %all-to-all-done.4 = bf16[32,2,512]{2,1,0:T(2,128)(2,1)S(1)} async-done(((bf16[32,2,512]{2,1,0:T(2,128)(2,1)}), bf16[32,2,512]{2,1,0:T(2,128)(2,1)S(1)}, u32[]{:S(2)}, u32[]{:S(2)}) %all-to-all-start.4) | async-done | bytes 65568 | tf_op jit(solution)/shard_map/all_to_all | solution.py:31
  45.5 0.7 broadcast_in_dim.8
  46.2 3.9 %all-to-all-start.1 = ((f32[32,1,1024]{2,1,0:T(1,128)}), f32[32,1,1024]{2,1,0:T(1,128)S(1)}, u32[]{:S(2)}, u32[]{:S(2)}) async-start(f32[32,1,1024]{2,1,0:T(1,128)} %broadcast_in_dim.8), calls=%async_computation.1 | async-start | bytes 262144 | tf_op jit(solution)/shard_map/all_to_all | solution.py:31
  50.3 0.2 broadcast_in_dim.10
  50.5 9.9 %all-to-all-done.1 = f32[32,1,1024]{2,1,0:T(1,128)S(1)} async-done(((f32[32,1,1024]{2,1,0:T(1,128)}), f32[32,1,1024]{2,1,0:T(1,128)S(1)}, u32[]{:S(2)}, u32[]{:S(2)}) %all-to-all-start.1) | async-done | bytes 131104 | tf_op jit(solution)/shard_map/all_to_all | solution.py:31
  60.4 0.7 broadcast_in_dim.11
  61.1 3.4 %all-to-all-start.5 = ((bf16[4,2048,16]{1,2,0:T(8,128)(2,1)}), bf16[4,2048,16]{1,2,0:T(8,128)(2,1)S(1)}, u32[]{:S(2)}, u32[]{:S(2)}) async-start(bf16[4,2048,16]{1,2,0:T(8,128)(2,1)} %broadcast_in_dim.11), calls=%async_computation.5 | async-start | bytes 524288 | tf_op jit(solution)/shard_map/all_to_all | solution.py:31
  64.5 0.2 slice_sqrt_fusion
  64.8 8.3 %divide_convert_fusion = (bf16[16,64,1024]{2,1,0:T(8,128)(2,1)}, bf16[16,64,1024]{2,1,0:T(8,128)(2,1)S(1)}) fusion(f32[16,1024]{1,0:T(8,128)S(1)} %get-tuple-element.11, f32[16,64,1024]{2,1,0:T(8,128)} %param.10, f32[16]{0:T(128)S(1)} %broadcast_subtract_fusion, f32[16,64,1024]{2,1,0:T(8,128)} %param.9, f32[16]{0:T(128)S(1)} %copy-done.1, ...), kind=kLoop, calls=%fused_computation | loop fusion | flops 10485760 | bytes 21102720 | tf_op jit(solution)/shard_map/convert_element_type | solution.py:64
  73.1 4.9 %copy.74 = bf16[16,64,1024]{1,0,2:T(8,128)(2,1)} copy(bf16[16,64,1024]{2,1,0:T(8,128)(2,1)S(1)} %get-tuple-element.10) | data formatting | bytes 4194304 | tf_op jit(solution)/shard_map/convert_element_type | solution.py:63
  78.0 7.9 %reshape.52 = bf16[32,2,16384]{2,1,0:T(2,128)(2,1)} reshape(bf16[1024,16,64]{2,1,0:T(8,128)(2,1)} %bitcast.32) | data formatting | bytes 4194304
  85.9 4.0 %all-to-all-start.2 = ((bf16[32,2,16384]{2,1,0:T(2,128)(2,1)}), bf16[32,2,16384]{2,1,0:T(2,128)(2,1)S(1)}, u32[]{:S(2)}, u32[]{:S(2)}) async-start(bf16[32,2,16384]{2,1,0:T(2,128)(2,1)} %reshape.52), calls=%async_computation.2 | async-start | bytes 4194304 | tf_op jit(solution)/shard_map/all_to_all | solution.py:67
  89.9 6.2 %copy.77 = bf16[16,64,1024]{1,0,2:T(8,128)(2,1)} copy(bf16[16,64,1024]{2,1,0:T(8,128)(2,1)} %get-tuple-element.9) | data formatting | bytes 4194304 | tf_op jit(solution)/shard_map/convert_element_type | solution.py:64
  96.1 7.9 %reshape.54 = bf16[32,2,16384]{2,1,0:T(2,128)(2,1)} reshape(bf16[1024,16,64]{2,1,0:T(8,128)(2,1)} %bitcast.33) | data formatting | bytes 4194304
  103.9 16.7 %all-to-all-done.2 = bf16[32,2,16384]{2,1,0:T(2,128)(2,1)S(1)} async-done(((bf16[32,2,16384]{2,1,0:T(2,128)(2,1)}), bf16[32,2,16384]{2,1,0:T(2,128)(2,1)S(1)}, u32[]{:S(2)}, u32[]{:S(2)}) %all-to-all-start.2) | async-done | bytes 2097184 | tf_op jit(solution)/shard_map/all_to_all | solution.py:67
  120.6 6.9 %all-to-all-start.3 = ((bf16[32,2,16384]{2,1,0:T(2,128)(2,1)}), bf16[32,2,16384]{2,1,0:T(2,128)(2,1)}, u32[]{:S(2)}, u32[]{:S(2)}) async-start(bf16[32,2,16384]{2,1,0:T(2,128)(2,1)} %reshape.54), calls=%async_computation.3 | async-start | bytes 4194304 | tf_op jit(solution)/shard_map/all_to_all | solution.py:68
  127.5 0.7 constant_dynamic-slice_fusion
  128.3 4.0 %reshape.53 = bf16[1024,16,64]{2,1,0:T(8,128)(2,1)} reshape(bf16[32,2,16384]{2,1,0:T(2,128)(2,1)S(1)} %all-to-all-done.2) | data formatting | bytes 4194304
  132.2 6.9 %copy.76 = bf16[16,32,64,32]{2,1,3,0:T(8,128)(2,1)} copy(bf16[16,32,64,32]{2,0,3,1:T(8,128)(2,1)} %bitcast.34) | data formatting | bytes 4194304 | tf_op jit(solution)/shard_map/all_to_all | solution.py:67
  139.1 6.7 %all_to_all.48 = bf16[16,2048,32]{1,2,0:T(8,128)(2,1)} reshape(bf16[16,32,64,32]{2,1,3,0:T(8,128)(2,1)} %copy.76) | data formatting | bytes 4194304 | tf_op jit(solution)/shard_map/all_to_all | solution.py:67
  145.9 11.4 %all-to-all-done.3 = bf16[32,2,16384]{2,1,0:T(2,128)(2,1)} async-done(((bf16[32,2,16384]{2,1,0:T(2,128)(2,1)}), bf16[32,2,16384]{2,1,0:T(2,128)(2,1)}, u32[]{:S(2)}, u32[]{:S(2)}) %all-to-all-start.3) | async-done | bytes 2097184 | tf_op jit(solution)/shard_map/all_to_all | solution.py:68
  157.3 7.9 %reshape.55 = bf16[1024,16,64]{2,1,0:T(8,128)(2,1)} reshape(bf16[32,2,16384]{2,1,0:T(2,128)(2,1)} %all-to-all-done.3) | data formatting | bytes 4194304
  165.2 6.9 %copy.79 = bf16[16,32,64,32]{2,1,3,0:T(8,128)(2,1)} copy(bf16[16,32,64,32]{2,0,3,1:T(8,128)(2,1)} %bitcast.35) | data formatting | bytes 4194304 | tf_op jit(solution)/shard_map/all_to_all | solution.py:68
  172.0 6.7 %all_to_all.52 = bf16[16,2048,32]{1,2,0:T(8,128)(2,1)} reshape(bf16[16,32,64,32]{2,1,3,0:T(8,128)(2,1)} %copy.79) | data formatting | bytes 4194304 | tf_op jit(solution)/shard_map/all_to_all | solution.py:68
  178.8 0.7 copy.90
  (14 shorter events, 0.3 us)
Async XLA Ops:
  1.3 20.1 %copy-start = (f32[64,16]{0,1:T(8,128)S(1)}, f32[64,16]{0,1:T(8,128)}, u32[]{:S(2)}) copy-start(f32[64,16]{0,1:T(8,128)} %param.12) | copy-start | bytes 12292
  1.3 20.1 %copy-start.2 = (f32[64]{0:T(128)S(1)}, f32[64]{0:T(128)}, u32[]{:S(2)}) copy-start(f32[64]{0:T(128)} %param.13) | copy-start | bytes 772
  1.3 63.5 %copy-start.1 = (f32[16]{0:T(128)S(1)}, f32[16]{0:T(128)}, u32[]{:S(2)}) copy-start(f32[16]{0:T(128)} %param.11) | copy-start | bytes 196
  10.5 21.2 %all-to-all-start = ((f32[32,1,1024]{2,1,0:T(1,128)}), f32[32,1,1024]{2,1,0:T(1,128)S(1)}, u32[]{:S(2)}, u32[]{:S(2)}) async-start(f32[32,1,1024]{2,1,0:T(1,128)} %all_to_all.42), calls=%async_computation | async-start | bytes 262144 | tf_op jit(solution)/shard_map/all_to_all | solution.py:14
  31.7 13.9 %all-to-all-start.4 = ((bf16[32,2,512]{2,1,0:T(2,128)(2,1)}), bf16[32,2,512]{2,1,0:T(2,128)(2,1)S(1)}, u32[]{:S(2)}, u32[]{:S(2)}) async-start(bf16[32,2,512]{2,1,0:T(2,128)(2,1)} %reshape.56), calls=%async_computation.4 | async-start | bytes 131072 | tf_op jit(solution)/shard_map/all_to_all | solution.py:31
  46.2 14.1 %all-to-all-start.1 = ((f32[32,1,1024]{2,1,0:T(1,128)}), f32[32,1,1024]{2,1,0:T(1,128)S(1)}, u32[]{:S(2)}, u32[]{:S(2)}) async-start(f32[32,1,1024]{2,1,0:T(1,128)} %broadcast_in_dim.8), calls=%async_computation.1 | async-start | bytes 262144 | tf_op jit(solution)/shard_map/all_to_all | solution.py:31
  61.1 24.8 %all-to-all-start.5 = ((bf16[4,2048,16]{1,2,0:T(8,128)(2,1)}), bf16[4,2048,16]{1,2,0:T(8,128)(2,1)S(1)}, u32[]{:S(2)}, u32[]{:S(2)}) async-start(bf16[4,2048,16]{1,2,0:T(8,128)(2,1)} %broadcast_in_dim.11), calls=%async_computation.5 | async-start | bytes 524288 | tf_op jit(solution)/shard_map/all_to_all | solution.py:31
  85.9 34.8 %all-to-all-start.2 = ((bf16[32,2,16384]{2,1,0:T(2,128)(2,1)}), bf16[32,2,16384]{2,1,0:T(2,128)(2,1)S(1)}, u32[]{:S(2)}, u32[]{:S(2)}) async-start(bf16[32,2,16384]{2,1,0:T(2,128)(2,1)} %reshape.52), calls=%async_computation.2 | async-start | bytes 4194304 | tf_op jit(solution)/shard_map/all_to_all | solution.py:67
  120.6 36.6 %all-to-all-start.3 = ((bf16[32,2,16384]{2,1,0:T(2,128)(2,1)}), bf16[32,2,16384]{2,1,0:T(2,128)(2,1)}, u32[]{:S(2)}, u32[]{:S(2)}) async-start(bf16[32,2,16384]{2,1,0:T(2,128)(2,1)} %reshape.54), calls=%async_computation.3 | async-start | bytes 4194304 | tf_op jit(solution)/shard_map/all_to_all | solution.py:68
where the time goes:
time: 182 us; the launch traced here: 179 us
  local copies, waits for them, and re-layouts  71 us (39%)
  waiting for transfers between devices  57.3 us (31%)
  starting transfers between devices  33 us (18%)
  other arithmetic  17.5 us (10%)
    unnamed x15, local copies, waits for them, and re-layouts  29.3 us
    all_to_all x3, waiting for transfers between devices, copy_for_each(): lax.all_to_all(jnp.broadcast_to(shard[None], (devices, *shard.shape)), ax...  19.8 us
    all_to_all x1, waiting for transfers between devices, body(): lax.all_to_all(narrow_gate, 'rows', split_axis=2, concat_axis=1, tiled=True)  16.7 us
    all_to_all x2, local copies, waits for them, and re-layouts, body(): lax.all_to_all(narrow_up, 'rows', split_axis=2, concat_axis=1, tiled=True)  13.6 us
    all_to_all x2, local copies, waits for them, and re-layouts, body(): lax.all_to_all(narrow_gate, 'rows', split_axis=2, concat_axis=1, tiled=True)  13.6 us
    all_to_all x1, waiting for transfers between devices, body(): lax.all_to_all(narrow_up, 'rows', split_axis=2, concat_axis=1, tiled=True)  11.4 us
    all_to_all x3, starting transfers between devices, copy_for_each(): lax.all_to_all(jnp.broadcast_to(shard[None], (devices, *shard.shape)), ax...  11.1 us
    all_to_all x1, starting transfers between devices, summed_on_arrival(): lax.all_to_all(cut_along(shard, dim, devices), axis, 0, 0, tiled=True)  10.9 us
  transfers between devices with their start and end apart: 6, of which 5 were waited for; matrix products, arithmetic and copies ran while one was open for 27% of the time, Pallas kernels for 0%

commit v1 on v0

v1 whole, which is shorter than its diff:
```python
import functools

import jax
import jax.numpy as jnp
from jax import lax
from jax.experimental import pallas as pl
from jax.experimental.pallas import tpu as pltpu
from jax.sharding import PartitionSpec as P

MESH = pl.DeviceIdType.MESH
SPAN = 252.0
LOW = 125.0
OFFSETS = [(a, b, c) for a in range(4) for b in range(2) for c in range(4)][1:]
NEAREST = sorted(OFFSETS, key=lambda o: min(o[0], 4 - o[0]) + 2 * o[1] + min(o[2], 4 - o[2]))


def left_half(shape):
    return lax.broadcasted_iota(jnp.int32, shape, len(shape) - 1) < 64


def swap_halves(a, b):
    left = left_half(a.shape)
    return jnp.where(left, a, pltpu.roll(b, 64, 1)), jnp.where(left, pltpu.roll(a, 64, 1), b)


def exchange(
    mix, w_gate, v_gate, w_up, v_up, weight, gain,
    out_gate, out_up, out_scale, out_router,
    w_in, v_in, peaks, sent, landed, sent_side, landed_side, side, spread, mixed, lines, scales,
    in_sem, send_sem, recv_sem, side_send, side_recv, line_send, line_recv,
):
    me, own = lax.axis_index("rows"), lax.axis_index("owner")
    z, y, x = me // 8, (me // 4) % 2, me % 4
    peers = [((z + a) % 4) * 8 + ((y + b) % 2) * 4 + (x + c) % 4 for a, b, c in NEAREST]
    sources = ((w_gate, v_gate), (w_up, v_up))

    def arrival(m, p, k):
        return pltpu.make_async_copy(
            sources[m][k].at[pl.ds(2 * p, 2)],
            (w_in, v_in)[k].at[m, pl.ds(2 * p, 2)],
            in_sem.at[m, p, k],
        )

    for m in range(2):
        for p in range(8):
            for k in range(2):
                arrival(m, p, k).start()

    barrier = pltpu.get_barrier_semaphore()
    for peer in peers:
        pl.semaphore_signal(barrier, inc=1, device_id=(own, peer), device_id_type=MESH)
    for step in range(1, 4):
        pl.semaphore_signal(
            barrier, inc=1, device_id=((own + step) % 4, me), device_id_type=MESH
        )

    for m in range(2):

        def code(p, carry, m=m):
            for k in range(2):
                arrival(m, p, k).wait()
            for q in range(8):
                cols = pl.ds(128 * q, 128)
                halves = []
                for h in range(2):
                    e = 2 * p + h
                    share = mix[e]
                    f = share * w_in[m, e, :, cols] + (1.0 - share) * v_in[m, e, :, cols]
                    size = jnp.abs(f)
                    peak = jnp.max(size, axis=0, keepdims=True)
                    peak = (peak * (1.0 + 2.0**-7)).astype(jnp.bfloat16).astype(jnp.float32)
                    peaks[16 * m + e, :, cols] = peak
                    rate = jnp.where(peak > 1e-30, SPAN / peak, 0.0)
                    level = jnp.exp2(size * rate - LOW)
                    halves.append(jnp.where(f < 0, -level, level))
                block = jnp.concatenate(halves, axis=0).T.astype(jnp.bfloat16)
                for r in range(4):
                    sent[8 * m + p, 4 * q + r] = block[32 * r : 32 * r + 32]
            landed[8 * m + p, me] = sent[8 * m + p, me]
            return carry

        lax.fori_loop(0, 8, code, 0)

    group = lax.broadcasted_iota(jnp.int32, (8, 128), 1) // 32
    routed = weight[...] * gain[...]
    routed = jnp.concatenate([routed[:8], routed[8:]], axis=1)
    for q in range(8):
        blocks = [peaks[8 * k : 8 * k + 8, 0, 128 * q : 128 * q + 128] for k in range(4)]
        for r in range(4):
            turned = blocks[r]
            for k in range(4):
                if k != r:
                    turned = jnp.where(
                        group == k, pltpu.roll(blocks[k], (32 * (k - r)) % 128, 1), turned
                    )
            sent_side[4 * q + r] = jnp.concatenate([turned, routed], axis=0).astype(jnp.bfloat16)
    landed_side[me] = sent_side[me]

    pl.semaphore_wait(barrier, 34)

    for peer in peers:
        pltpu.make_async_remote_copy(
            src_ref=sent_side.at[peer], dst_ref=landed_side.at[me],
            send_sem=side_send, recv_sem=side_recv,
            device_id=(own, peer), device_id_type=MESH,
        ).start()

    def ship(c, carry):
        for peer in peers:
            pltpu.make_async_remote_copy(
                src_ref=sent.at[c, peer], dst_ref=landed.at[c, me],
                send_sem=send_sem.at[c], recv_sem=recv_sem.at[c],
                device_id=(own, peer), device_id_type=MESH,
            ).start()
        return carry

    lax.fori_loop(0, 16, ship, 0)

    def all_side():
        return pltpu.make_async_remote_copy(
            src_ref=sent_side.at[pl.ds(0, 31)], dst_ref=landed_side.at[pl.ds(0, 31)],
            send_sem=side_send, recv_sem=side_recv, device_id=(own, peers[0]), device_id_type=MESH,
        )

    def all_codes(c):
        return pltpu.make_async_remote_copy(
            src_ref=sent.at[c, pl.ds(0, 31)], dst_ref=landed.at[c, pl.ds(0, 31)],
            send_sem=send_sem.at[c], recv_sem=recv_sem.at[c],
            device_id=(own, peers[0]), device_id_type=MESH,
        )

    all_side().wait_recv()
    side[...] = landed_side[...].astype(jnp.float32)

    for k in range(16):
        for h, block in enumerate(swap_halves(side[2 * k, 8:, :], side[2 * k + 1, 8:, :])):
            lines[own, 8 * h : 8 * h + 8, 128 * k : 128 * k + 128] = block.astype(jnp.bfloat16)

    def pass_on(step):
        return pltpu.make_async_remote_copy(
            src_ref=lines.at[own], dst_ref=lines.at[own],
            send_sem=line_send.at[step - 1], recv_sem=line_recv.at[step - 1],
            device_id=((own + step) % 4, me), device_id_type=MESH,
        )

    for step in range(1, 4):
        pass_on(step).start()

    at = lax.broadcasted_iota(jnp.int32, (32, 2048), 1) // 64
    picks = (at == lax.broadcasted_iota(jnp.int32, (32, 2048), 0)).astype(jnp.bfloat16)
    for r in range(8):
        turned = side[:, r, :].T.astype(jnp.bfloat16)
        spread[r] = jnp.dot(turned, picks, preferred_element_type=jnp.float32)

    scales[...] = jnp.zeros_like(scales)
    for m, out in enumerate((out_gate, out_up)):

        def decode(p, carry, m=m, out=out):
            c = 8 * m + p
            all_codes(c).wait_recv()
            rows = []
            for h in range(2):
                e = 2 * p + h
                rows.append((e % 8, pl.ds(pl.multiple_of(32 * (2 * m + e // 8), 32), 32)))
            sums = [jnp.zeros((32, 128), jnp.float32)] * 2
            for k in range(16):
                levels = []
                for s in range(2):
                    block = landed[c, 2 * k + s].astype(jnp.float32)
                    size = jnp.log2(jnp.abs(block)) + LOW
                    levels.append(jnp.where(block < 0, -size, size))
                for h, level in enumerate(swap_halves(*levels)):
                    f = level * spread[rows[h][0], rows[h][1], 128 * k : 128 * k + 128]
                    sums[h] += f * f
                    mixed[h, :, 128 * k : 128 * k + 128] = f
            lane = lax.broadcasted_iota(jnp.int32, (32, 128), 1)
            for h in range(2):
                e = 2 * p + h
                scale = jnp.sqrt(jnp.sum(sums[h], axis=1, keepdims=True))
                scales[...] = jnp.where(lane == 16 * m + e, scale * (1.0 / SPAN), scales[...])
                out[e] = (mixed[h] * (1.0 / scale)).astype(jnp.bfloat16)
            return carry

        lax.fori_loop(0, 8, decode, 0)

    out_scale[...] = scales[...].T[:32]

    for step in range(1, 4):
        pass_on(step).wait()
    for o in range(4):
        out_router[16 * o : 16 * o + 16] = lines[o]

    all_side().wait_send()

    def drain(c, carry):
        all_codes(c).wait_send()
        return carry

    lax.fori_loop(0, 16, drain, 0)


def body(w_gate, avg_gate, w_up, avg_up, mix_share, router_weight, router_gain):
    vmem = pl.BlockSpec(memory_space=pltpu.VMEM)
    hbm = pl.BlockSpec(memory_space=pl.ANY)
    f32, bf16 = jnp.float32, jnp.bfloat16
    serve_gate, serve_up, scale, router = pl.pallas_call(
        exchange,
        out_shape=[
            jax.ShapeDtypeStruct((16, 32, 2048), bf16),
            jax.ShapeDtypeStruct((16, 32, 2048), bf16),
            jax.ShapeDtypeStruct((32, 32), f32),
            jax.ShapeDtypeStruct((64, 2048), bf16),
        ],
        in_specs=[pl.BlockSpec(memory_space=pltpu.SMEM), hbm, hbm, hbm, hbm, vmem, vmem],
        out_specs=[vmem] * 4,
        scratch_shapes=[
            pltpu.VMEM((2, 16, 64, 1024), f32),
            pltpu.VMEM((2, 16, 64, 1024), f32),
            pltpu.VMEM((32, 1, 1024), f32),
            pltpu.VMEM((16, 32, 32, 128), bf16),
            pltpu.VMEM((16, 32, 32, 128), bf16),
            pltpu.VMEM((32, 16, 128), bf16),
            pltpu.VMEM((32, 16, 128), bf16),
            pltpu.VMEM((32, 16, 128), f32),
            pltpu.VMEM((8, 128, 2048), f32),
            pltpu.VMEM((2, 32, 2048), f32),
            pltpu.VMEM((4, 16, 2048), bf16),
            pltpu.VMEM((32, 128), f32),
            pltpu.SemaphoreType.DMA((2, 8, 2)),
            pltpu.SemaphoreType.DMA((16,)),
            pltpu.SemaphoreType.DMA((16,)),
            pltpu.SemaphoreType.DMA,
            pltpu.SemaphoreType.DMA,
            pltpu.SemaphoreType.DMA((3,)),
            pltpu.SemaphoreType.DMA((3,)),
        ],
        compiler_params=pltpu.CompilerParams(
            collective_id=0, has_side_effects=True, vmem_limit_bytes=56 << 20
        ),
        name="exchange",
    )(
        mix_share, w_gate, avg_gate, w_up, avg_up, router_weight.T, router_gain.reshape(1, 64)
    )
    return (
        jnp.swapaxes(serve_gate, 1, 2),
        jnp.swapaxes(serve_up, 1, 2),
        scale[:16],
        scale[16:],
        router.T,
    )


def solution(mesh):
    return jax.shard_map(
        body,
        mesh=mesh,
        in_specs=(
            P("owner", "rows", None),
            P("owner", "rows", None),
            P("owner", "rows", None),
            P("owner", "rows", None),
            P("owner"),
            P("rows", "owner"),
            P("rows"),
        ),
        out_specs=(
            P("owner", None, "rows"),
            P("owner", None, "rows"),
            P("owner", "rows"),
            P("owner", "rows"),
            P(),
        ),
        check_vma=False,
    )
```

time: 182 us -> 74.3 us (0.41); the launches traced: 179 us -> 74.1 us
  Pallas kernels: 0 us -> 66.8 us
  local copies, waits for them, and re-layouts: 71 us -> 6.7 us
  waiting for transfers between devices: 57.3 us -> 0 us
  starting transfers between devices: 33 us -> 0 us
  other arithmetic: 17.5 us -> 0 us
    pallas_call x0 -> x1, Pallas kernels: none -> 66.8 us  [body(): pl.pallas_call(exchange, out_shape=[jax.ShapeDtypeStruct((16, 32, 2048),...]
    all_to_all x6 -> x0, waiting for transfers between devices: 57.3 us -> none  [the longest x3 19.8 us: copy_for_each(): lax.all_to_all(jnp.broadcast_to(shard[None], (devices, *shard.shape)), ax...]
    all_to_all x6 -> x0, starting transfers between devices: 33 us -> none  [the longest x3 11.1 us: copy_for_each(): lax.all_to_all(jnp.broadcast_to(shard[None], (devices, *shard.shape)), ax...]
    all_to_all x6 -> x0, local copies, waits for them, and re-layouts: 28 us -> none  [the longest x2 13.6 us: body(): lax.all_to_all(narrow_up, 'rows', split_axis=2, concat_axis=1, tiled=True)]
    unnamed x15 -> x7, local copies, waits for them, and re-layouts: 29.3 us -> 5.23 us
    convert_element_type x2 -> x0, local copies, waits for them, and re-layouts: 11.1 us -> none  [the longest x1 6.2 us: body(): (fresh_up / jnp.expand_dims(scale_up, 1)).astype(jnp.bfloat16)]
    reduce_sum x2 -> x0, other arithmetic: 8.52 us -> none  [the longest x1 8.42 us: body(): jnp.sum(fresh_gate * fresh_gate, axis=1)]
    convert_element_type x2 -> x0, other arithmetic: 8.31 us -> none  [the longest x1 8.31 us: body(): (fresh_up / jnp.expand_dims(scale_up, 1)).astype(jnp.bfloat16)]
  transfers between devices with their start and end apart: 6 -> 0, of which waited for: 5 -> 0; matrix products, arithmetic and copies ran while one was open for 27% -> 0% of each run, Pallas kernels for 0% -> 0%
where the time goes in v1:
time: 74.3 us; the launch traced here: 74.1 us
  Pallas kernels  66.8 us (90%)
  local copies, waits for them, and re-layouts  6.7 us (9%)
    pallas_call x1, Pallas kernels, body(): pl.pallas_call(exchange, out_shape=[jax.ShapeDtypeStruct((16, 32, 2048),...  66.8 us
    unnamed x7, local copies, waits for them, and re-layouts  5.23 us

profile of v1, /device:TPU:0, one launch (start us, length us, event | category | flops | bytes accessed | tf_op | source)
XLA Modules:
  0.0 74.1 jit_solution(12322576183442179354)
XLA Ops:
  0.6 66.8 %exchange.1 = (bf16[16,32,2048]{2,1,0:T(8,128)(2,1)}, bf16[16,32,2048]{2,1,0:T(8,128)(2,1)}, f32[32,32]{1,0:T(8,128)}, bf16[64,2048]{1,0:T(8,128)(2,1)}) custom-call(f32[16]{0:T(128)} %mix.1, f32[16,64,1024]{2,1,0:T(8,128)} %w_gate.1, f32[16,64,1024]{2,1,0:T(8,128)} %v_gate.1, f32[16,64,1024]{2,1,0:T(8,128)} %w_up.1, f32[16,64,1024]{2,1,0:T(8,128)} %v_up.1, ...), custom_call_target="tpu_custom_call" | custom-call | tf_op jit(solution)/shard_map/exchange/pallas_call | solution.py:206
  67.4 0.0 copy-start
  67.4 1.5 %fusion = (f32[16,32]{1,0:T(8,128)}, f32[16,32]{1,0:T(8,128)}) fusion(f32[32,32]{1,0:T(8,128)} %get-tuple-element.11), kind=kLoop, calls=%fused_computation | loop fusion | bytes 8192 | tf_op jit(solution)/shard_map/slice | solution.py:248
  68.9 0.0 copy-start.1
  68.9 3.2 %copy.15 = bf16[16,2048,32]{1,2,0:T(8,128)(2,1)} copy(bf16[16,2048,32]{1,2,0:T(8,128)(2,1)} %bitcast.6) | data formatting | bytes 4194304
  72.1 0.0 copy-done
  72.1 1.3 %copy.16 = bf16[16,2048,32]{1,2,0:T(8,128)(2,1)} copy(bf16[16,2048,32]{1,2,0:T(8,128)(2,1)S(1)} %bitcast.5) | data formatting | bytes 4194304
  73.4 0.0 copy-done.1
  73.4 0.7 copy.17
Async XLA Ops:
  67.4 4.7 %copy-start = (bf16[16,32,2048]{2,1,0:T(8,128)(2,1)S(1)}, bf16[16,32,2048]{2,1,0:T(8,128)(2,1)}, u32[]{:S(2)}) copy-start(bf16[16,32,2048]{2,1,0:T(8,128)(2,1)} %get-tuple-element.10) | copy-start | bytes 6291460
  68.9 4.5 %copy-start.1 = (bf16[64,2048]{1,0:T(8,128)(2,1)S(1)}, bf16[64,2048]{1,0:T(8,128)(2,1)}, u32[]{:S(2)}) copy-start(bf16[64,2048]{1,0:T(8,128)(2,1)} %get-tuple-element.12) | copy-start | bytes 786436

commit v2 on v1

--- a/solution.py
+++ b/solution.py
@@ -10,6 +10,9 @@
 MESH = pl.DeviceIdType.MESH
 SPAN = 252.0
 LOW = 125.0
+AHEAD = 4
+FIRST = 4
+SECOND = 12
 OFFSETS = [(a, b, c) for a in range(4) for b in range(2) for c in range(4)][1:]
 NEAREST = sorted(OFFSETS, key=lambda o: min(o[0], 4 - o[0]) + 2 * o[1] + min(o[2], 4 - o[2]))
 
@@ -24,14 +27,21 @@
 
 
 def exchange(
-    mix, w_gate, v_gate, w_up, v_up, weight, gain,
-    out_gate, out_up, out_scale, out_router,
-    w_in, v_in, peaks, sent, landed, sent_side, landed_side, side, spread, mixed, lines, scales,
-    in_sem, send_sem, recv_sem, side_send, side_recv, line_send, line_recv,
+    mix_hbm, w_gate, v_gate, w_up, v_up, weight_hbm, gain_hbm,
+    out_gate, out_up, out_scale_gate, out_scale_up, out_router,
+    mix, weight, gain, w_in, v_in, peaks, sent, landed, sent_side, landed_side, side, spread, mixed, lines, scales,
+    small_sem, in_sem, send_sem, recv_sem, side_send, side_recv, line_send, line_recv,
 ):
     me, own = lax.axis_index("rows"), lax.axis_index("owner")
     z, y, x = me // 8, (me // 4) % 2, me % 4
     peers = [((z + a) % 4) * 8 + ((y + b) % 2) * 4 + (x + c) % 4 for a, b, c in NEAREST]
+    half = own // 2
+    across = (own + 2) % 4
+    beside = [
+        (across, z * 8 + ((y + half) % 2) * 4 + x),
+        (across, z * 8 + ((y + 1 - half) % 2) * 4 + x),
+        (own + 1 - 2 * (own % 2), me),
+    ]
     sources = ((w_gate, v_gate), (w_up, v_up))
 
     def arrival(m, p, k):
@@ -41,45 +51,72 @@
             in_sem.at[m, p, k],
         )
 
-    for m in range(2):
-        for p in range(8):
+    barrier = pltpu.get_barrier_semaphore()
+    for peer in reversed(peers):
+        pl.semaphore_signal(barrier, inc=1, device_id=(own, peer), device_id_type=MESH)
+    for other in beside:
+        pl.semaphore_signal(barrier, inc=1, device_id=other, device_id_type=MESH)
+
+    small = [
+        pltpu.make_async_copy(a, b, small_sem.at[i])
+        for i, (a, b) in enumerate(((mix_hbm, mix), (weight_hbm, weight), (gain_hbm, gain)))
+    ]
+    for copy in small:
+        copy.start()
+    for p in range(AHEAD):
+        for k in range(2):
+            arrival(0, p, k).start()
+
+    for copy in small:
+        copy.wait()
+
+    def code(m, p, ahead):
+        if ahead is not None:
             for k in range(2):
-                arrival(m, p, k).start()
-
-    barrier = pltpu.get_barrier_semaphore()
-    for peer in peers:
-        pl.semaphore_signal(barrier, inc=1, device_id=(own, peer), device_id_type=MESH)
-    for step in range(1, 4):
-        pl.semaphore_signal(
-            barrier, inc=1, device_id=((own + step) % 4, me), device_id_type=MESH
-        )
-
-    for m in range(2):
-
-        def code(p, carry, m=m):
-            for k in range(2):
-                arrival(m, p, k).wait()
-            for q in range(8):
-                cols = pl.ds(128 * q, 128)
-                halves = []
-                for h in range(2):
-                    e = 2 * p + h
-                    share = mix[e]
-                    f = share * w_in[m, e, :, cols] + (1.0 - share) * v_in[m, e, :, cols]
-                    size = jnp.abs(f)
-                    peak = jnp.max(size, axis=0, keepdims=True)
-                    peak = (peak * (1.0 + 2.0**-7)).astype(jnp.bfloat16).astype(jnp.float32)
-                    peaks[16 * m + e, :, cols] = peak
-                    rate = jnp.where(peak > 1e-30, SPAN / peak, 0.0)
-                    level = jnp.exp2(size * rate - LOW)
-                    halves.append(jnp.where(f < 0, -level, level))
-                block = jnp.concatenate(halves, axis=0).T.astype(jnp.bfloat16)
-                for r in range(4):
-                    sent[8 * m + p, 4 * q + r] = block[32 * r : 32 * r + 32]
-            landed[8 * m + p, me] = sent[8 * m + p, me]
+                arrival(ahead, (p + AHEAD) % 8, k).start()
+        for k in range(2):
+            arrival(m, p, k).wait()
+        for q in range(8):
+            cols = pl.ds(128 * q, 128)
+            halves = []
+            for h in range(2):
+                e = 2 * p + h
+                share = mix[e]
+                f = share * w_in[m, e, :, cols] + (1.0 - share) * v_in[m, e, :, cols]
+                size = jnp.abs(f)
+                peak = jnp.max(size, axis=0, keepdims=True)
+                peak = (peak * (1.0 + 2.0**-7)).astype(jnp.bfloat16).astype(jnp.float32)
+                peaks[16 * m + e, :, cols] = peak
+                rate = jnp.where(peak > 1e-30, SPAN / peak, 0.0)
+                level = jnp.exp2(size * rate - LOW)
+                halves.append(jnp.where(f < 0, -level, level))
+            block = jnp.concatenate(halves, axis=0).T.astype(jnp.bfloat16)
+            for r in range(4):
+                sent[8 * m + p, 4 * q + r] = block[32 * r : 32 * r + 32]
+        landed[8 * m + p, me] = sent[8 * m + p, me]
+
+    def code_all(m, begin, end, ahead):
+        def step(p, carry):
+            code(m, p, ahead)
             return carry
 
-        lax.fori_loop(0, 8, code, 0)
+        lax.fori_loop(begin, end, step, 0)
+
+    def ship(c, carry):
+        for peer in peers:
+            pltpu.make_async_remote_copy(
+                src_ref=sent.at[c, peer], dst_ref=landed.at[c, me],
+                send_sem=send_sem.at[c], recv_sem=recv_sem.at[c],
+                device_id=(own, peer), device_id_type=MESH,
+            ).start()
+        return carry
+
+    code_all(0, 0, 4, 0)
+    pl.semaphore_wait(barrier, 34)
+    lax.fori_loop(0, FIRST, ship, 0)
+    code_all(0, 4, 8, 1)
+    code_all(1, 0, 4, 1)
+    code_all(1, 4, 8, None)
 
     group = lax.broadcasted_iota(jnp.int32, (8, 128), 1) // 32
     routed = weight[...] * gain[...]
@@ -96,8 +133,6 @@
             sent_side[4 * q + r] = jnp.concatenate([turned, routed], axis=0).astype(jnp.bfloat16)
     landed_side[me] = sent_side[me]
 
-    pl.semaphore_wait(barrier, 34)
-
     for peer in peers:
         pltpu.make_async_remote_copy(
             src_ref=sent_side.at[peer], dst_ref=landed_side.at[me],
@@ -105,16 +140,7 @@
             device_id=(own, peer), device_id_type=MESH,
         ).start()
 
-    def ship(c, carry):
-        for peer in peers:
-            pltpu.make_async_remote_copy(
-                src_ref=sent.at[c, peer], dst_ref=landed.at[c, me],
-                send_sem=send_sem.at[c], recv_sem=recv_sem.at[c],
-                device_id=(own, peer), device_id_type=MESH,
-            ).start()
-        return carry
-
-    lax.fori_loop(0, 16, ship, 0)
+    lax.fori_loop(FIRST, SECOND, ship, 0)
 
     def all_side():
         return pltpu.make_async_remote_copy(
@@ -136,15 +162,22 @@
         for h, block in enumerate(swap_halves(side[2 * k, 8:, :], side[2 * k + 1, 8:, :])):
             lines[own, 8 * h : 8 * h + 8, 128 * k : 128 * k + 128] = block.astype(jnp.bfloat16)
 
-    def pass_on(step):
+    def pass_on(n, block, columns, to):
         return pltpu.make_async_remote_copy(
-            src_ref=lines.at[own], dst_ref=lines.at[own],
-            send_sem=line_send.at[step - 1], recv_sem=line_recv.at[step - 1],
-            device_id=((own + step) % 4, me), device_id_type=MESH,
+            src_ref=lines.at[block, :, columns], dst_ref=lines.at[block, :, columns],
+            send_sem=line_send.at[n], recv_sem=line_recv.at[n],
+            device_id=to, device_id_type=MESH,
         )
 
-    for step in range(1, 4):
-        pass_on(step).start()
+    whole = pl.ds(0, 2048)
+    upward = pass_on(0, own, pl.ds(0, 1024), beside[0])
+    downward = pass_on(1, own, pl.ds(1024, 1024), beside[1])
+    over = pass_on(2, own, whole, beside[2])
+    relay = pass_on(3, across, whole, beside[2])
+    for copy in (upward, downward, over):
+        copy.start()
+
+    lax.fori_loop(SECOND, 16, ship, 0)
 
     at = lax.broadcasted_iota(jnp.int32, (32, 2048), 1) // 64
     picks = (at == lax.broadcasted_iota(jnp.int32, (32, 2048), 0)).astype(jnp.bfloat16)
@@ -181,12 +214,23 @@
                 out[e] = (mixed[h] * (1.0 / scale)).astype(jnp.bfloat16)
             return carry
 
-        lax.fori_loop(0, 8, decode, 0)
-
-    out_scale[...] = scales[...].T[:32]
-
-    for step in range(1, 4):
-        pass_on(step).wait()
+        if m == 0:
+            lax.fori_loop(0, 8, decode, 0)
+        else:
+            lax.fori_loop(0, 5, decode, 0)
+            upward.wait_recv()
+            downward.wait_recv()
+            relay.start()
+            lax.fori_loop(5, 8, decode, 0)
+
+    turned = scales[...].T
+    out_scale_gate[...] = turned[:16]
+    out_scale_up[...] = turned[16:32]
+
+    over.wait()
+    relay.wait()
+    upward.wait_send()
+    downward.wait_send()
     for o in range(4):
         out_router[16 * o : 16 * o + 16] = lines[o]
 
@@ -199,21 +243,38 @@
     lax.fori_loop(0, 16, drain, 0)
 
 
+def write_out(*refs):
+    sems = refs[-1]
+    n = (len(refs) - 1) // 2
+    copies = [
+        pltpu.make_async_copy(refs[i], refs[n + i], sems.at[i]) for i in range(n)
+    ]
+    for copy in copies:
+        copy.start()
+    for copy in copies:
+        copy.wait()
+
+
 def body(w_gate, avg_gate, w_up, avg_up, mix_share, router_weight, router_gain):
     vmem = pl.BlockSpec(memory_space=pltpu.VMEM)
-    hbm = pl.BlockSpec(memory_space=pl.ANY)
+    hbm = pl.BlockSpec(memory_space=pltpu.HBM)
     f32, bf16 = jnp.float32, jnp.bfloat16
-    serve_gate, serve_up, scale, router = pl.pallas_call(
+    shapes = [
+        ((16, 32, 2048), bf16),
+        ((16, 32, 2048), bf16),
+        ((16, 32), f32),
+        ((16, 32), f32),
+        ((64, 2048), bf16),
+    ]
+    results = pl.pallas_call(
         exchange,
-        out_shape=[
-            jax.ShapeDtypeStruct((16, 32, 2048), bf16),
-            jax.ShapeDtypeStruct((16, 32, 2048), bf16),
-            jax.ShapeDtypeStruct((32, 32), f32),
-            jax.ShapeDtypeStruct((64, 2048), bf16),
-        ],
-        in_specs=[pl.BlockSpec(memory_space=pltpu.SMEM), hbm, hbm, hbm, hbm, vmem, vmem],
-        out_specs=[vmem] * 4,
+        out_shape=[pltpu.VMEM(*shape) for shape in shapes],
+        in_specs=[hbm] * 7,
+        out_specs=[vmem] * 5,
         scratch_shapes=[
+            pltpu.SMEM((16,), f32),
+            pltpu.VMEM((16, 64), f32),
+            pltpu.VMEM((1, 64), f32),
             pltpu.VMEM((2, 16, 64, 1024), f32),
             pltpu.VMEM((2, 16, 64, 1024), f32),
             pltpu.VMEM((32, 1, 1024), f32),
@@ -226,26 +287,42 @@
             pltpu.VMEM((2, 32, 2048), f32),
             pltpu.VMEM((4, 16, 2048), bf16),
             pltpu.VMEM((32, 128), f32),
+            pltpu.SemaphoreType.DMA((3,)),
             pltpu.SemaphoreType.DMA((2, 8, 2)),
             pltpu.SemaphoreType.DMA((16,)),
             pltpu.SemaphoreType.DMA((16,)),
             pltpu.SemaphoreType.DMA,
             pltpu.SemaphoreType.DMA,
-            pltpu.SemaphoreType.DMA((3,)),
-            pltpu.SemaphoreType.DMA((3,)),
+            pltpu.SemaphoreType.DMA((4,)),
+            pltpu.SemaphoreType.DMA((4,)),
         ],
         compiler_params=pltpu.CompilerParams(
-            collective_id=0, has_side_effects=True, vmem_limit_bytes=56 << 20
+            collective_id=0, has_side_effects=True, vmem_limit_bytes=40 << 20
         ),
         name="exchange",
     )(
-        mix_share, w_gate, avg_gate, w_up, avg_up, router_weight.T, router_gain.reshape(1, 64)
+        *[
+            pltpu.with_memory_space_constraint(a, pltpu.HBM)
+            for a in (
+                mix_share, w_gate, avg_gate, w_up, avg_up,
+                router_weight.T, router_gain.reshape(1, 64),
+            )
+        ]
     )
+    serve_gate, serve_up, scale_gate, scale_up, router = pl.pallas_call(
+        write_out,
+        out_shape=[jax.ShapeDtypeStruct(*shape) for shape in shapes],
+        in_specs=[vmem] * 5,
+        out_specs=[hbm] * 5,
+        scratch_shapes=[pltpu.SemaphoreType.DMA((5,))],
+        compiler_params=pltpu.CompilerParams(vmem_limit_bytes=4 << 20),
+        name="write_out",
+    )(*[pltpu.with_memory_space_constraint(a, pltpu.VMEM) for a in results])
     return (
         jnp.swapaxes(serve_gate, 1, 2),
         jnp.swapaxes(serve_up, 1, 2),
-        scale[:16],
-        scale[16:],
+        scale_gate,
+        scale_up,
         router.T,
     )
 

time: 74.3 us -> 64 us (0.86)
  local copies, waits for them, and re-layouts: 6.7 us -> 0 us
  Pallas kernels: 66.8 us -> 63.2 us
    unnamed x7 -> x0, local copies, waits for them, and re-layouts: 5.23 us -> none
    pallas_call x1 -> x2, Pallas kernels: 66.8 us -> 63.2 us  [the longest x1 61.1 us: body(): pl.pallas_call(exchange, out_shape=[pltpu.VMEM(*shape) for shape in shape...]
    slice x1 -> x0, local copies, waits for them, and re-layouts: 1.47 us -> none  [body(): scale[16:]]
where the time goes in v2:
time: 64 us; the launch traced here: 63.9 us
  Pallas kernels  63.2 us (99%)
  between operations  0.64 us (1%)
    pallas_call x1, Pallas kernels, body(): pl.pallas_call(exchange, out_shape=[pltpu.VMEM(*shape) for shape in shape...  61.1 us
    pallas_call x1, Pallas kernels, body(): pl.pallas_call(write_out, out_shape=[jax.ShapeDtypeStruct(*shape) for sha...  2.14 us

profile of v2, /device:TPU:0, one launch (start us, length us, event | category | flops | bytes accessed | tf_op | source)
XLA Modules:
  0.0 63.9 jit_solution(13067340599497099932)
XLA Ops:
  0.6 61.1 %exchange.1 = (bf16[16,32,2048]{2,1,0:T(8,128)(2,1)S(1)}, bf16[16,32,2048]{2,1,0:T(8,128)(2,1)S(1)}, f32[16,32]{1,0:T(8,128)S(1)}, f32[16,32]{1,0:T(8,128)S(1)}, bf16[64,2048]{1,0:T(8,128)(2,1)S(1)}) custom-call(f32[16]{0:T(128)} %mix_hbm.1, f32[16,64,1024]{2,1,0:T(8,128)} %w_gate.1, f32[16,64,1024]{2,1,0:T(8,128)} %v_gate.1, f32[16,64,1024]{2,1,0:T(8,128)} %w_up.1, ...), custom_call_target="tpu_custom_call" | custom-call | tf_op jit(solution)/shard_map/exchange/pallas_call | solution.py:269
  61.7 2.1 %write_out.1 = (bf16[16,32,2048]{2,1,0:T(8,128)(2,1)}, bf16[16,32,2048]{2,1,0:T(8,128)(2,1)}, f32[16,32]{1,0:T(8,128)}, f32[16,32]{1,0:T(8,128)}, bf16[64,2048]{1,0:T(8,128)(2,1)}) custom-call(bf16[16,32,2048]{2,1,0:T(8,128)(2,1)S(1)} %get-tuple-element.15.refs_0_, bf16[16,32,2048]{2,1,0:T(8,128)(2,1)S(1)} %get-tuple-element.16.refs_1_, ...), custom_call_target="tpu_custom_call" | custom-call | tf_op jit(solution)/shard_map/write_out/pallas_call | solution.py:312

commit v3 on v2

--- a/solution.py
+++ b/solution.py
@@ -61,14 +61,14 @@
         pltpu.make_async_copy(a, b, small_sem.at[i])
         for i, (a, b) in enumerate(((mix_hbm, mix), (weight_hbm, weight), (gain_hbm, gain)))
     ]
-    for copy in small:
-        copy.start()
+    small[0].start()
     for p in range(AHEAD):
         for k in range(2):
             arrival(0, p, k).start()
-
-    for copy in small:
-        copy.wait()
+    for copy in small[1:]:
+        copy.start()
+
+    small[0].wait()
 
     def code(m, p, ahead):
         if ahead is not None:
@@ -111,14 +111,22 @@
             ).start()
         return carry
 
-    code_all(0, 0, 4, 0)
+    code_all(0, 0, 1, 0)
     pl.semaphore_wait(barrier, 34)
-    lax.fori_loop(0, FIRST, ship, 0)
+    ship(0, 0)
+
+    def code_and_ship(p, carry):
+        code(0, p, 0)
+        return ship(p, carry)
+
+    lax.fori_loop(1, FIRST, code_and_ship, 0)
     code_all(0, 4, 8, 1)
     code_all(1, 0, 4, 1)
     code_all(1, 4, 8, None)
 
     group = lax.broadcasted_iota(jnp.int32, (8, 128), 1) // 32
+    for copy in small[1:]:
+        copy.wait()
     routed = weight[...] * gain[...]
     routed = jnp.concatenate([routed[:8], routed[8:]], axis=1)
     for q in range(8):

time: 64 us -> 62.7 us (0.980)
  Pallas kernels: 63.2 us -> 61.9 us
    pallas_call x1, Pallas kernels: 61.1 us -> 59.8 us  [body(): pl.pallas_call(exchange, out_shape=[pltpu.VMEM(*shape) for shape in shape...]
where the time goes in v3:
time: 62.7 us; the launch traced here: 62.5 us
  Pallas kernels  61.9 us (99%)
  between operations  0.64 us (1%)
    pallas_call x1, Pallas kernels, body(): pl.pallas_call(exchange, out_shape=[pltpu.VMEM(*shape) for shape in shape...  59.8 us
    pallas_call x1, Pallas kernels, body(): pl.pallas_call(write_out, out_shape=[jax.ShapeDtypeStruct(*shape) for sha...  2.14 us

profile of v3, /device:TPU:0, one launch (start us, length us, event | category | flops | bytes accessed | tf_op | source)
XLA Modules:
  0.0 62.5 jit_solution(12886721437987348480)
XLA Ops:
  0.6 59.8 %exchange.1 = (bf16[16,32,2048]{2,1,0:T(8,128)(2,1)S(1)}, bf16[16,32,2048]{2,1,0:T(8,128)(2,1)S(1)}, f32[16,32]{1,0:T(8,128)S(1)}, f32[16,32]{1,0:T(8,128)S(1)}, bf16[64,2048]{1,0:T(8,128)(2,1)S(1)}) custom-call(f32[16]{0:T(128)} %mix_hbm.1, f32[16,64,1024]{2,1,0:T(8,128)} %w_gate.1, f32[16,64,1024]{2,1,0:T(8,128)} %v_gate.1, f32[16,64,1024]{2,1,0:T(8,128)} %w_up.1, ...), custom_call_target="tpu_custom_call" | custom-call | tf_op jit(solution)/shard_map/exchange/pallas_call | solution.py:277
  60.4 2.1 %write_out.1 = (bf16[16,32,2048]{2,1,0:T(8,128)(2,1)}, bf16[16,32,2048]{2,1,0:T(8,128)(2,1)}, f32[16,32]{1,0:T(8,128)}, f32[16,32]{1,0:T(8,128)}, bf16[64,2048]{1,0:T(8,128)(2,1)}) custom-call(bf16[16,32,2048]{2,1,0:T(8,128)(2,1)S(1)} %get-tuple-element.15.refs_0_, bf16[16,32,2048]{2,1,0:T(8,128)(2,1)S(1)} %get-tuple-element.16.refs_1_, ...), custom_call_target="tpu_custom_call" | custom-call | tf_op jit(solution)/shard_map/write_out/pallas_call | solution.py:320

commit v4 on v3

--- a/solution.py
+++ b/solution.py
@@ -14,7 +14,7 @@
 FIRST = 4
 SECOND = 12
 OFFSETS = [(a, b, c) for a in range(4) for b in range(2) for c in range(4)][1:]
-NEAREST = sorted(OFFSETS, key=lambda o: min(o[0], 4 - o[0]) + 2 * o[1] + min(o[2], 4 - o[2]))
+FARTHEST = sorted(OFFSETS, key=lambda o: -min(o[0], 4 - o[0]) - 2 * o[1] - min(o[2], 4 - o[2]))
 
 
 def left_half(shape):
@@ -33,14 +33,17 @@
     small_sem, in_sem, send_sem, recv_sem, side_send, side_recv, line_send, line_recv,
 ):
     me, own = lax.axis_index("rows"), lax.axis_index("owner")
-    z, y, x = me // 8, (me // 4) % 2, me % 4
-    peers = [((z + a) % 4) * 8 + ((y + b) % 2) * 4 + (x + c) % 4 for a, b, c in NEAREST]
-    half = own // 2
-    across = (own + 2) % 4
+    z, y, x = lax.div(me, 8), lax.rem(lax.div(me, 4), 2), lax.rem(me, 4)
+    zs = [lax.rem(z + a, 4) * 8 for a in range(4)]
+    ys = [y * 4, (1 - y) * 4]
+    xs = [lax.rem(x + c, 4) for c in range(4)]
+    peers = [zs[a] + ys[b] + xs[c] for a, b, c in FARTHEST]
+    half = lax.div(own, 2)
+    across = lax.rem(own + 2, 4)
     beside = [
-        (across, z * 8 + ((y + half) % 2) * 4 + x),
-        (across, z * 8 + ((y + 1 - half) % 2) * 4 + x),
-        (own + 1 - 2 * (own % 2), me),
+        (across, z * 8 + lax.rem(y + half, 2) * 4 + x),
+        (across, z * 8 + lax.rem(y + 1 - half, 2) * 4 + x),
+        (own + 1 - 2 * lax.rem(own, 2), me),
     ]
     sources = ((w_gate, v_gate), (w_up, v_up))
 
@@ -48,11 +51,11 @@
         return pltpu.make_async_copy(
             sources[m][k].at[pl.ds(2 * p, 2)],
             (w_in, v_in)[k].at[m, pl.ds(2 * p, 2)],
-            in_sem.at[m, p, k],
+            in_sem.at[(p % AHEAD) if isinstance(p, int) else lax.rem(p, AHEAD), k],
         )
 
     barrier = pltpu.get_barrier_semaphore()
-    for peer in reversed(peers):
+    for peer in peers:
         pl.semaphore_signal(barrier, inc=1, device_id=(own, peer), device_id_type=MESH)
     for other in beside:
         pl.semaphore_signal(barrier, inc=1, device_id=other, device_id_type=MESH)
@@ -71,11 +74,11 @@
     small[0].wait()
 
     def code(m, p, ahead):
+        for k in range(2):
+            arrival(m, p, k).wait()
         if ahead is not None:
             for k in range(2):
-                arrival(ahead, (p + AHEAD) % 8, k).start()
-        for k in range(2):
-            arrival(m, p, k).wait()
+                arrival(ahead, lax.rem(p + AHEAD, 8), k).start()
         for q in range(8):
             cols = pl.ds(128 * q, 128)
             halves = []
@@ -106,7 +109,7 @@
         for peer in peers:
             pltpu.make_async_remote_copy(
                 src_ref=sent.at[c, peer], dst_ref=landed.at[c, me],
-                send_sem=send_sem.at[c], recv_sem=recv_sem.at[c],
+                send_sem=send_sem, recv_sem=recv_sem.at[c],
                 device_id=(own, peer), device_id_type=MESH,
             ).start()
         return carry
@@ -159,7 +162,7 @@
     def all_codes(c):
         return pltpu.make_async_remote_copy(
             src_ref=sent.at[c, pl.ds(0, 31)], dst_ref=landed.at[c, pl.ds(0, 31)],
-            send_sem=send_sem.at[c], recv_sem=recv_sem.at[c],
+            send_sem=send_sem, recv_sem=recv_sem.at[c],
             device_id=(own, peers[0]), device_id_type=MESH,
         )
 
@@ -244,11 +247,11 @@
 
     all_side().wait_send()
 
-    def drain(c, carry):
-        all_codes(c).wait_send()
-        return carry
-
-    lax.fori_loop(0, 16, drain, 0)
+    pltpu.make_async_remote_copy(
+        src_ref=sent.at[:, pl.ds(0, 31)], dst_ref=landed.at[:, pl.ds(0, 31)],
+        send_sem=send_sem, recv_sem=recv_sem.at[0],
+        device_id=(own, peers[0]), device_id_type=MESH,
+    ).wait_send()
 
 
 def write_out(*refs):
@@ -296,8 +299,8 @@
             pltpu.VMEM((4, 16, 2048), bf16),
             pltpu.VMEM((32, 128), f32),
             pltpu.SemaphoreType.DMA((3,)),
-            pltpu.SemaphoreType.DMA((2, 8, 2)),
-            pltpu.SemaphoreType.DMA((16,)),
+            pltpu.SemaphoreType.DMA((AHEAD, 2)),
+            pltpu.SemaphoreType.DMA,
             pltpu.SemaphoreType.DMA((16,)),
             pltpu.SemaphoreType.DMA,
             pltpu.SemaphoreType.DMA,

time: 62.7 us -> 62 us (0.989)
  Pallas kernels: 61.9 us -> 61.2 us
    pallas_call x1, Pallas kernels: 59.8 us -> 59.1 us  [body(): pl.pallas_call(exchange, out_shape=[pltpu.VMEM(*shape) for shape in shape...]
where the time goes in v4:
time: 62 us; the launch traced here: 61.9 us
  Pallas kernels  61.2 us (99%)
  between operations  0.64 us (1%)
    pallas_call x1, Pallas kernels, body(): pl.pallas_call(exchange, out_shape=[pltpu.VMEM(*shape) for shape in shape...  59.1 us
    pallas_call x1, Pallas kernels, body(): pl.pallas_call(write_out, out_shape=[jax.ShapeDtypeStruct(*shape) for sha...  2.14 us

profile of v4, /device:TPU:0, one launch (start us, length us, event | category | flops | bytes accessed | tf_op | source)
XLA Modules:
  0.0 61.9 jit_solution(6875044287849698086)
XLA Ops:
  0.6 59.1 %exchange.1 = (bf16[16,32,2048]{2,1,0:T(8,128)(2,1)S(1)}, bf16[16,32,2048]{2,1,0:T(8,128)(2,1)S(1)}, f32[16,32]{1,0:T(8,128)S(1)}, f32[16,32]{1,0:T(8,128)S(1)}, bf16[64,2048]{1,0:T(8,128)(2,1)S(1)}) custom-call(f32[16]{0:T(128)} %mix_hbm.1, f32[16,64,1024]{2,1,0:T(8,128)} %w_gate.1, f32[16,64,1024]{2,1,0:T(8,128)} %v_gate.1, f32[16,64,1024]{2,1,0:T(8,128)} %w_up.1, ...), custom_call_target="tpu_custom_call" | custom-call | tf_op jit(solution)/shard_map/exchange/pallas_call | solution.py:280
  59.7 2.1 %write_out.1 = (bf16[16,32,2048]{2,1,0:T(8,128)(2,1)}, bf16[16,32,2048]{2,1,0:T(8,128)(2,1)}, f32[16,32]{1,0:T(8,128)}, f32[16,32]{1,0:T(8,128)}, bf16[64,2048]{1,0:T(8,128)(2,1)}) custom-call(bf16[16,32,2048]{2,1,0:T(8,128)(2,1)S(1)} %get-tuple-element.15.refs_0_, bf16[16,32,2048]{2,1,0:T(8,128)(2,1)S(1)} %get-tuple-element.16.refs_1_, ...), custom_call_target="tpu_custom_call" | custom-call | tf_op jit(solution)/shard_map/write_out/pallas_call | solution.py:323

commit v5 on v4

--- a/solution.py
+++ b/solution.py
@@ -12,7 +12,8 @@
 LOW = 125.0
 AHEAD = 4
 FIRST = 4
-SECOND = 12
+SECOND = 8
+THIRD = 12
 OFFSETS = [(a, b, c) for a in range(4) for b in range(2) for c in range(4)][1:]
 FARTHEST = sorted(OFFSETS, key=lambda o: -min(o[0], 4 - o[0]) - 2 * o[1] - min(o[2], 4 - o[2]))
 
@@ -29,8 +30,8 @@
 def exchange(
     mix_hbm, w_gate, v_gate, w_up, v_up, weight_hbm, gain_hbm,
     out_gate, out_up, out_scale_gate, out_scale_up, out_router,
-    mix, weight, gain, w_in, v_in, peaks, sent, landed, sent_side, landed_side, side, spread, mixed, lines, scales,
-    small_sem, in_sem, send_sem, recv_sem, side_send, side_recv, line_send, line_recv,
+    mix, weight, gain, w_in, v_in, peaks, sent, landed, sent_side, landed_side, side, spread, mixed, gathered, lines, scales,
+    small_sem, in_sem, send_sem, recv_sem, side_send, side_recv, gather_send, gather_recv, line_send, line_recv,
 ):
     me, own = lax.axis_index("rows"), lax.axis_index("owner")
     z, y, x = lax.div(me, 8), lax.rem(lax.div(me, 4), 2), lax.rem(me, 4)
@@ -105,6 +106,18 @@
 
         lax.fori_loop(begin, end, step, 0)
 
+    def gather(n, part, to):
+        return pltpu.make_async_remote_copy(
+            src_ref=part, dst_ref=part, send_sem=gather_send.at[n], recv_sem=gather_recv.at[n],
+            device_id=(own, to), device_id_type=MESH,
+        )
+
+    along_y = gather(0, gathered.at[z, x, y], zs[0] + ys[1] + x)
+    along_x = [gather(1, gathered.at[z, x], zs[0] + ys[0] + xs[c]) for c in (2, 1, 3)]
+    along_z = [gather(2, gathered.at[z], zs[a] + ys[0] + x) for a in (2, 1, 3)]
+    all_x = gather(1, gathered.at[0, pl.ds(0, 3)], peers[0])
+    all_z = gather(2, gathered.at[pl.ds(0, 3)], peers[0])
+
     def ship(c, carry):
         for peer in peers:
             pltpu.make_async_remote_copy(
@@ -115,7 +128,13 @@
         return carry
 
     code_all(0, 0, 1, 0)
+    for copy in small[1:]:
+        copy.wait()
+    block = weight[...] * gain[...]
+    block = jnp.concatenate([block[:8], block[8:]], axis=1)
+    gathered[z, x, y] = block.astype(jnp.bfloat16)
     pl.semaphore_wait(barrier, 34)
+    along_y.start()
     ship(0, 0)
 
     def code_and_ship(p, carry):
@@ -126,12 +145,11 @@
     code_all(0, 4, 8, 1)
     code_all(1, 0, 4, 1)
     code_all(1, 4, 8, None)
+    along_y.wait_recv()
+    for copy in along_x:
+        copy.start()
 
     group = lax.broadcasted_iota(jnp.int32, (8, 128), 1) // 32
-    for copy in small[1:]:
-        copy.wait()
-    routed = weight[...] * gain[...]
-    routed = jnp.concatenate([routed[:8], routed[8:]], axis=1)
     for q in range(8):
         blocks = [peaks[8 * k : 8 * k + 8, 0, 128 * q : 128 * q + 128] for k in range(4)]
         for r in range(4):
@@ -141,7 +159,7 @@
                     turned = jnp.where(
                         group == k, pltpu.roll(blocks[k], (32 * (k - r)) % 128, 1), turned
                     )
-            sent_side[4 * q + r] = jnp.concatenate([turned, routed], axis=0).astype(jnp.bfloat16)
+            sent_side[4 * q + r] = turned.astype(jnp.bfloat16)
     landed_side[me] = sent_side[me]
 
     for peer in peers:
@@ -168,10 +186,10 @@
 
     all_side().wait_recv()
     side[...] = landed_side[...].astype(jnp.float32)
-
-    for k in range(16):
-        for h, block in enumerate(swap_halves(side[2 * k, 8:, :], side[2 * k + 1, 8:, :])):
-            lines[own, 8 * h : 8 * h + 8, 128 * k : 128 * k + 128] = block.astype(jnp.bfloat16)
+    all_x.wait_recv()
+    for copy in along_z:
+        copy.start()
+    lax.fori_loop(SECOND, THIRD, ship, 0)
 
     def pass_on(n, block, columns, to):
         return pltpu.make_async_remote_copy(
@@ -185,10 +203,19 @@
     downward = pass_on(1, own, pl.ds(1024, 1024), beside[1])
     over = pass_on(2, own, whole, beside[2])
     relay = pass_on(3, across, whole, beside[2])
-    for copy in (upward, downward, over):
-        copy.start()
-
-    lax.fori_loop(SECOND, 16, ship, 0)
+
+    def pass_router():
+        all_z.wait_recv()
+        for k in range(16):
+            pair = [
+                gathered[k // 4, 2 * (k % 2) + h, (k // 2) % 2].astype(jnp.float32)
+                for h in range(2)
+            ]
+            for h, block in enumerate(swap_halves(*pair)):
+                lines[own, 8 * h : 8 * h + 8, 128 * k : 128 * k + 128] = block.astype(jnp.bfloat16)
+        for copy in (upward, downward, over):
+            copy.start()
+        lax.fori_loop(THIRD, 16, ship, 0)
 
     at = lax.broadcasted_iota(jnp.int32, (32, 2048), 1) // 64
     picks = (at == lax.broadcasted_iota(jnp.int32, (32, 2048), 0)).astype(jnp.bfloat16)
@@ -226,7 +253,9 @@
             return carry
 
         if m == 0:
-            lax.fori_loop(0, 8, decode, 0)
+            lax.fori_loop(0, 6, decode, 0)
+            pass_router()
+            lax.fori_loop(6, 8, decode, 0)
         else:
             lax.fori_loop(0, 5, decode, 0)
             upward.wait_recv()
@@ -238,6 +267,9 @@
     out_scale_gate[...] = turned[:16]
     out_scale_up[...] = turned[16:32]
 
+    along_y.wait_send()
+    all_x.wait_send()
+    all_z.wait_send()
     over.wait()
     relay.wait()
     upward.wait_send()
@@ -291,11 +323,12 @@
             pltpu.VMEM((32, 1, 1024), f32),
             pltpu.VMEM((16, 32, 32, 128), bf16),
             pltpu.VMEM((16, 32, 32, 128), bf16),
-            pltpu.VMEM((32, 16, 128), bf16),
-            pltpu.VMEM((32, 16, 128), bf16),
-            pltpu.VMEM((32, 16, 128), f32),
+            pltpu.VMEM((32, 8, 128), bf16),
+            pltpu.VMEM((32, 8, 128), bf16),
+            pltpu.VMEM((32, 8, 128), f32),
             pltpu.VMEM((8, 128, 2048), f32),
             pltpu.VMEM((2, 32, 2048), f32),
+            pltpu.VMEM((4, 4, 2, 8, 128), bf16),
             pltpu.VMEM((4, 16, 2048), bf16),
             pltpu.VMEM((32, 128), f32),
             pltpu.SemaphoreType.DMA((3,)),
@@ -304,6 +337,8 @@
             pltpu.SemaphoreType.DMA((16,)),
             pltpu.SemaphoreType.DMA,
             pltpu.SemaphoreType.DMA,
+            pltpu.SemaphoreType.DMA((3,)),
+            pltpu.SemaphoreType.DMA((3,)),
             pltpu.SemaphoreType.DMA((4,)),
             pltpu.SemaphoreType.DMA((4,)),
         ],

time: 62 us -> 61.5 us (level)
  no operation moved by 1% of the time
where the time goes in v5:
time: 61.5 us; the launch traced here: 61.3 us
  Pallas kernels  60.7 us (99%)
  between operations  0.64 us (1%)
    pallas_call x1, Pallas kernels, body(): pl.pallas_call(exchange, out_shape=[pltpu.VMEM(*shape) for shape in shape...  58.5 us
    pallas_call x1, Pallas kernels, body(): pl.pallas_call(write_out, out_shape=[jax.ShapeDtypeStruct(*shape) for sha...  2.14 us

profile of v5, /device:TPU:0, one launch (start us, length us, event | category | flops | bytes accessed | tf_op | source)
XLA Modules:
  0.0 61.3 jit_solution(16053567986115231346)
XLA Ops:
  0.6 58.5 %exchange.1 = (bf16[16,32,2048]{2,1,0:T(8,128)(2,1)S(1)}, bf16[16,32,2048]{2,1,0:T(8,128)(2,1)S(1)}, f32[16,32]{1,0:T(8,128)S(1)}, f32[16,32]{1,0:T(8,128)S(1)}, bf16[64,2048]{1,0:T(8,128)(2,1)S(1)}) custom-call(f32[16]{0:T(128)} %mix_hbm.1, f32[16,64,1024]{2,1,0:T(8,128)} %w_gate.1, f32[16,64,1024]{2,1,0:T(8,128)} %v_gate.1, f32[16,64,1024]{2,1,0:T(8,128)} %w_up.1, ...), custom_call_target="tpu_custom_call" | custom-call | tf_op jit(solution)/shard_map/exchange/pallas_call | solution.py:312
  59.2 2.1 %write_out.1 = (bf16[16,32,2048]{2,1,0:T(8,128)(2,1)}, bf16[16,32,2048]{2,1,0:T(8,128)(2,1)}, f32[16,32]{1,0:T(8,128)}, f32[16,32]{1,0:T(8,128)}, bf16[64,2048]{1,0:T(8,128)(2,1)}) custom-call(bf16[16,32,2048]{2,1,0:T(8,128)(2,1)S(1)} %get-tuple-element.15.refs_0_, bf16[16,32,2048]{2,1,0:T(8,128)(2,1)S(1)} %get-tuple-element.16.refs_1_, ...), custom_call_target="tpu_custom_call" | custom-call | tf_op jit(solution)/shard_map/write_out/pallas_call | solution.py:358

commit v6 on v5

--- a/solution.py
+++ b/solution.py
@@ -27,10 +27,25 @@
     return jnp.where(left, a, pltpu.roll(b, 64, 1)), jnp.where(left, pltpu.roll(a, 64, 1), b)
 
 
+def decode_pair(code, spread, mixed):
+    sums = [jnp.zeros((32, 128), jnp.float32)] * 2
+    for k in range(16):
+        levels = []
+        for s in range(2):
+            block = code(2 * k + s).astype(jnp.float32)
+            size = jnp.log2(jnp.abs(block)) + LOW
+            levels.append(jnp.where(block < 0, -size, size))
+        for h, level in enumerate(swap_halves(*levels)):
+            f = level * spread(h, pl.ds(128 * k, 128))
+            sums[h] += f * f
+            mixed[h, :, 128 * k : 128 * k + 128] = f
+    return [jnp.sqrt(jnp.sum(total, axis=1, keepdims=True)) for total in sums]
+
+
 def exchange(
     mix_hbm, w_gate, v_gate, w_up, v_up, weight_hbm, gain_hbm,
-    out_gate, out_up, out_scale_gate, out_scale_up, out_router,
-    mix, weight, gain, w_in, v_in, peaks, sent, landed, sent_side, landed_side, side, spread, mixed, gathered, lines, scales,
+    out_gate, out_up, out_router, scales, last_codes, last_spread,
+    mix, weight, gain, w_in, v_in, peaks, sent, landed, sent_side, landed_side, side, spread, mixed, gathered, lines,
     small_sem, in_sem, send_sem, recv_sem, side_send, side_recv, gather_send, gather_recv, line_send, line_recv,
 ):
     me, own = lax.axis_index("rows"), lax.axis_index("owner")
@@ -223,31 +238,27 @@
         turned = side[:, r, :].T.astype(jnp.bfloat16)
         spread[r] = jnp.dot(turned, picks, preferred_element_type=jnp.float32)
 
+    def peak_rows(m, e):
+        start = 32 * (2 * m + lax.div(e, 8))
+        return lax.rem(e, 8), pl.ds(start if isinstance(start, int) else pl.multiple_of(start, 32), 32)
+
+    for h in range(2):
+        last_spread[h] = spread[6 + h, 96:128, :]
+
     scales[...] = jnp.zeros_like(scales)
     for m, out in enumerate((out_gate, out_up)):
 
         def decode(p, carry, m=m, out=out):
             c = 8 * m + p
             all_codes(c).wait_recv()
-            rows = []
-            for h in range(2):
+            found = decode_pair(
+                lambda source: landed[c, source],
+                lambda h, lanes: spread[peak_rows(m, 2 * p + h) + (lanes,)],
+                mixed,
+            )
+            lane = lax.broadcasted_iota(jnp.int32, (32, 128), 1)
+            for h, scale in enumerate(found):
                 e = 2 * p + h
-                rows.append((e % 8, pl.ds(pl.multiple_of(32 * (2 * m + e // 8), 32), 32)))
-            sums = [jnp.zeros((32, 128), jnp.float32)] * 2
-            for k in range(16):
-                levels = []
-                for s in range(2):
-                    block = landed[c, 2 * k + s].astype(jnp.float32)
-                    size = jnp.log2(jnp.abs(block)) + LOW
-                    levels.append(jnp.where(block < 0, -size, size))
-                for h, level in enumerate(swap_halves(*levels)):
-                    f = level * spread[rows[h][0], rows[h][1], 128 * k : 128 * k + 128]
-                    sums[h] += f * f
-                    mixed[h, :, 128 * k : 128 * k + 128] = f
-            lane = lax.broadcasted_iota(jnp.int32, (32, 128), 1)
-            for h in range(2):
-                e = 2 * p + h
-                scale = jnp.sqrt(jnp.sum(sums[h], axis=1, keepdims=True))
                 scales[...] = jnp.where(lane == 16 * m + e, scale * (1.0 / SPAN), scales[...])
                 out[e] = (mixed[h] * (1.0 / scale)).astype(jnp.bfloat16)
             return carry
@@ -261,11 +272,7 @@
             upward.wait_recv()
             downward.wait_recv()
             relay.start()
-            lax.fori_loop(5, 8, decode, 0)
-
-    turned = scales[...].T
-    out_scale_gate[...] = turned[:16]
-    out_scale_up[...] = turned[16:32]
+            lax.fori_loop(5, 7, decode, 0)
 
     along_y.wait_send()
     all_x.wait_send()
@@ -278,6 +285,8 @@
         out_router[16 * o : 16 * o + 16] = lines[o]
 
     all_side().wait_send()
+    all_codes(15).wait_recv()
+    last_codes[...] = landed[15]
 
     pltpu.make_async_remote_copy(
         src_ref=sent.at[:, pl.ds(0, 31)], dst_ref=landed.at[:, pl.ds(0, 31)],
@@ -286,13 +295,29 @@
     ).wait_send()
 
 
-def write_out(*refs):
-    sems = refs[-1]
-    n = (len(refs) - 1) // 2
-    copies = [
-        pltpu.make_async_copy(refs[i], refs[n + i], sems.at[i]) for i in range(n)
-    ]
-    for copy in copies:
+def write_out(
+    gate, up, router, scales, last_codes, last_spread,
+    out_gate, out_up, out_scale_gate, out_scale_up, out_router,
+    mixed, last, scale_gate, scale_up, sems,
+):
+    early = [(gate, out_gate), (up.at[:14], out_up.at[:14]), (router, out_router)]
+    late = [(last, out_up.at[14:]), (scale_gate, out_scale_gate), (scale_up, out_scale_up)]
+    copies = [pltpu.make_async_copy(a, b, sems.at[i]) for i, (a, b) in enumerate(early + late)]
+    for copy in copies[:3]:
+        copy.start()
+    found = decode_pair(
+        lambda source: last_codes[source], lambda h, lanes: last_spread[h, :, lanes], mixed
+    )
+    lane = lax.broadcasted_iota(jnp.int32, (32, 128), 1)
+    table = scales[...]
+    for h, scale in enumerate(found):
+        table = jnp.where(lane == 30 + h, scale * (1.0 / SPAN), table)
+        last[h] = (mixed[h] * (1.0 / scale)).astype(jnp.bfloat16)
+    copies[3].start()
+    turned = table.T
+    scale_gate[...] = turned[:16]
+    scale_up[...] = turned[16:32]
+    for copy in copies[4:]:
         copy.start()
     for copy in copies:
         copy.wait()
@@ -302,18 +327,14 @@
     vmem = pl.BlockSpec(memory_space=pltpu.VMEM)
     hbm = pl.BlockSpec(memory_space=pltpu.HBM)
     f32, bf16 = jnp.float32, jnp.bfloat16
-    shapes = [
-        ((16, 32, 2048), bf16),
-        ((16, 32, 2048), bf16),
-        ((16, 32), f32),
-        ((16, 32), f32),
-        ((64, 2048), bf16),
-    ]
+    codes = [((16, 32, 2048), bf16), ((16, 32, 2048), bf16), ((64, 2048), bf16)]
+    carried = codes + [((32, 128), f32), ((32, 32, 128), bf16), ((2, 32, 2048), f32)]
+    shapes = codes[:2] + [((16, 32), f32), ((16, 32), f32), codes[2]]
     results = pl.pallas_call(
         exchange,
-        out_shape=[pltpu.VMEM(*shape) for shape in shapes],
+        out_shape=[pltpu.VMEM(*shape) for shape in carried],
         in_specs=[hbm] * 7,
-        out_specs=[vmem] * 5,
+        out_specs=[vmem] * 6,
         scratch_shapes=[
             pltpu.SMEM((16,), f32),
             pltpu.VMEM((16, 64), f32),
@@ -330,7 +351,6 @@
             pltpu.VMEM((2, 32, 2048), f32),
             pltpu.VMEM((4, 4, 2, 8, 128), bf16),
             pltpu.VMEM((4, 16, 2048), bf16),
-            pltpu.VMEM((32, 128), f32),
             pltpu.SemaphoreType.DMA((3,)),
             pltpu.SemaphoreType.DMA((AHEAD, 2)),
             pltpu.SemaphoreType.DMA,
@@ -358,9 +378,15 @@
     serve_gate, serve_up, scale_gate, scale_up, router = pl.pallas_call(
         write_out,
         out_shape=[jax.ShapeDtypeStruct(*shape) for shape in shapes],
-        in_specs=[vmem] * 5,
+        in_specs=[vmem] * 6,
         out_specs=[hbm] * 5,
-        scratch_shapes=[pltpu.SemaphoreType.DMA((5,))],
+        scratch_shapes=[
+            pltpu.VMEM((2, 32, 2048), f32),
+            pltpu.VMEM((2, 32, 2048), bf16),
+            pltpu.VMEM((16, 32), f32),
+            pltpu.VMEM((16, 32), f32),
+            pltpu.SemaphoreType.DMA((6,)),
+        ],
         compiler_params=pltpu.CompilerParams(vmem_limit_bytes=4 << 20),
         name="write_out",
     )(*[pltpu.with_memory_space_constraint(a, pltpu.VMEM) for a in results])

time: 61.5 us -> 61.1 us (level)
  no operation moved by 1% of the time
where the time goes in v6:
time: 61.1 us; the launch traced here: 60.9 us
  Pallas kernels  60.3 us (99%)
  between operations  0.64 us (1%)
    pallas_call x1, Pallas kernels, body(): pl.pallas_call(exchange, out_shape=[pltpu.VMEM(*shape) for shape in carri...  58.1 us
    pallas_call x1, Pallas kernels, body(): pl.pallas_call(write_out, out_shape=[jax.ShapeDtypeStruct(*shape) for sha...  2.14 us

profile of v6, /device:TPU:0, one launch (start us, length us, event | category | flops | bytes accessed | tf_op | source)
XLA Modules:
  0.0 60.9 jit_solution(3047105372744226821)
XLA Ops:
  0.6 58.1 %exchange.1 = (bf16[16,32,2048]{2,1,0:T(8,128)(2,1)S(1)}, bf16[16,32,2048]{2,1,0:T(8,128)(2,1)S(1)}, bf16[64,2048]{1,0:T(8,128)(2,1)S(1)}, f32[32,128]{1,0:T(8,1...) custom-call(f32[16]{0:T(128)} %mix_hbm.1, f32[16,64,1024]{2,1,0:T(8,128)} %w_gate.1, ...), custom_call_target="tpu_custom_call" | custom-call | tf_op jit(solution)/shard_map/exchange/pallas_call | solution.py:333
  58.8 2.1 %write_out.1 = (bf16[16,32,2048]{2,1,0:T(8,128)(2,1)}, bf16[16,32,2048]{2,1,0:T(8,128)(2,1)}, f32[16,32]{1,0:T(8,128)}, f32[16,32]{1,0:T(8,128)}, bf16[64,2048]{1,0:T(8,128)(2,1)}) custom-call(bf16[16,32,2048]{2,1,0:T(8,128)(2,1)S(1)} %get-tuple-element.16.gate, bf16[16,32,2048]{2,1,0:T(8,128)(2,1)S(1)} %get-tuple-element.17.up, ...), custom_call_target="tpu_custom_call" | custom-call | tf_op jit(solution)/shard_map/write_out/pallas_call | solution.py:378

commit v7 on v6

--- a/solution.py
+++ b/solution.py
@@ -14,6 +14,7 @@
 FIRST = 4
 SECOND = 8
 THIRD = 12
+LATE = 14
 OFFSETS = [(a, b, c) for a in range(4) for b in range(2) for c in range(4)][1:]
 FARTHEST = sorted(OFFSETS, key=lambda o: -min(o[0], 4 - o[0]) - 2 * o[1] - min(o[2], 4 - o[2]))
 
@@ -230,7 +231,14 @@
                 lines[own, 8 * h : 8 * h + 8, 128 * k : 128 * k + 128] = block.astype(jnp.bfloat16)
         for copy in (upward, downward, over):
             copy.start()
-        lax.fori_loop(THIRD, 16, ship, 0)
+        lax.fori_loop(THIRD, LATE, ship, 0)
+        for peer in peers:
+            for c in range(LATE, 16):
+                pltpu.make_async_remote_copy(
+                    src_ref=sent.at[c, peer], dst_ref=landed.at[c, me],
+                    send_sem=send_sem, recv_sem=recv_sem.at[c],
+                    device_id=(own, peer), device_id_type=MESH,
+                ).start()
 
     at = lax.broadcasted_iota(jnp.int32, (32, 2048), 1) // 64
     picks = (at == lax.broadcasted_iota(jnp.int32, (32, 2048), 0)).astype(jnp.bfloat16)
@@ -242,8 +250,8 @@
         start = 32 * (2 * m + lax.div(e, 8))
         return lax.rem(e, 8), pl.ds(start if isinstance(start, int) else pl.multiple_of(start, 32), 32)
 
-    for h in range(2):
-        last_spread[h] = spread[6 + h, 96:128, :]
+    for h in range(4):
+        last_spread[h] = spread[4 + h, 96:128, :]
 
     scales[...] = jnp.zeros_like(scales)
     for m, out in enumerate((out_gate, out_up)):
@@ -272,7 +280,7 @@
             upward.wait_recv()
             downward.wait_recv()
             relay.start()
-            lax.fori_loop(5, 7, decode, 0)
+            lax.fori_loop(5, 6, decode, 0)
 
     along_y.wait_send()
     all_x.wait_send()
@@ -285,8 +293,9 @@
         out_router[16 * o : 16 * o + 16] = lines[o]
 
     all_side().wait_send()
-    all_codes(15).wait_recv()
-    last_codes[...] = landed[15]
+    for c in range(LATE, 16):
+        all_codes(c).wait_recv()
+        last_codes[c - LATE] = landed[c]
 
     pltpu.make_async_remote_copy(
         src_ref=sent.at[:, pl.ds(0, 31)], dst_ref=landed.at[:, pl.ds(0, 31)],
@@ -300,24 +309,28 @@
     out_gate, out_up, out_scale_gate, out_scale_up, out_router,
     mixed, last, scale_gate, scale_up, sems,
 ):
-    early = [(gate, out_gate), (up.at[:14], out_up.at[:14]), (router, out_router)]
-    late = [(last, out_up.at[14:]), (scale_gate, out_scale_gate), (scale_up, out_scale_up)]
+    early = [(gate, out_gate), (up.at[:12], out_up.at[:12]), (router, out_router)]
+    late = [(last.at[2 * n : 2 * n + 2], out_up.at[12 + 2 * n : 14 + 2 * n]) for n in range(2)]
+    late += [(scale_gate, out_scale_gate), (scale_up, out_scale_up)]
     copies = [pltpu.make_async_copy(a, b, sems.at[i]) for i, (a, b) in enumerate(early + late)]
     for copy in copies[:3]:
         copy.start()
-    found = decode_pair(
-        lambda source: last_codes[source], lambda h, lanes: last_spread[h, :, lanes], mixed
-    )
     lane = lax.broadcasted_iota(jnp.int32, (32, 128), 1)
     table = scales[...]
-    for h, scale in enumerate(found):
-        table = jnp.where(lane == 30 + h, scale * (1.0 / SPAN), table)
-        last[h] = (mixed[h] * (1.0 / scale)).astype(jnp.bfloat16)
-    copies[3].start()
+    for n in range(2):
+        found = decode_pair(
+            lambda source: last_codes[n, source],
+            lambda h, lanes: last_spread[2 * n + h, :, lanes],
+            mixed,
+        )
+        for h, scale in enumerate(found):
+            table = jnp.where(lane == 28 + 2 * n + h, scale * (1.0 / SPAN), table)
+            last[2 * n + h] = (mixed[h] * (1.0 / scale)).astype(jnp.bfloat16)
+        copies[3 + n].start()
     turned = table.T
     scale_gate[...] = turned[:16]
     scale_up[...] = turned[16:32]
-    for copy in copies[4:]:
+    for copy in copies[5:]:
         copy.start()
     for copy in copies:
         copy.wait()
@@ -328,7 +341,7 @@
     hbm = pl.BlockSpec(memory_space=pltpu.HBM)
     f32, bf16 = jnp.float32, jnp.bfloat16
     codes = [((16, 32, 2048), bf16), ((16, 32, 2048), bf16), ((64, 2048), bf16)]
-    carried = codes + [((32, 128), f32), ((32, 32, 128), bf16), ((2, 32, 2048), f32)]
+    carried = codes + [((32, 128), f32), ((2, 32, 32, 128), bf16), ((4, 32, 2048), f32)]
     shapes = codes[:2] + [((16, 32), f32), ((16, 32), f32), codes[2]]
     results = pl.pallas_call(
         exchange,
@@ -382,10 +395,10 @@
         out_specs=[hbm] * 5,
         scratch_shapes=[
             pltpu.VMEM((2, 32, 2048), f32),
-            pltpu.VMEM((2, 32, 2048), bf16),
+            pltpu.VMEM((4, 32, 2048), bf16),
             pltpu.VMEM((16, 32), f32),
             pltpu.VMEM((16, 32), f32),
-            pltpu.SemaphoreType.DMA((6,)),
+            pltpu.SemaphoreType.DMA((7,)),
         ],
         compiler_params=pltpu.CompilerParams(vmem_limit_bytes=4 << 20),
         name="write_out",

time: 61.1 us -> 60.8 us (level)
  no operation moved by 1% of the time
where the time goes in v7:
time: 60.8 us; the launch traced here: 60.6 us
  Pallas kernels  60 us (99%)
  between operations  0.64 us (1%)
    pallas_call x1, Pallas kernels, body(): pl.pallas_call(exchange, out_shape=[pltpu.VMEM(*shape) for shape in carri...  57.8 us
    pallas_call x1, Pallas kernels, body(): pl.pallas_call(write_out, out_shape=[jax.ShapeDtypeStruct(*shape) for sha...  2.15 us

profile of v7, /device:TPU:0, one launch (start us, length us, event | category | flops | bytes accessed | tf_op | source)
XLA Modules:
  0.0 60.6 jit_solution(14493855740796692422)
XLA Ops:
  0.6 57.8 %exchange.1 = (bf16[16,32,2048]{2,1,0:T(8,128)(2,1)S(1)}, bf16[16,32,2048]{2,1,0:T(8,128)(2,1)S(1)}, bf16[64,2048]{1,0:T(8,128)(2,1)S(1)}, f32[32,128]{1,0:T(8,1...) custom-call(f32[16]{0:T(128)} %mix_hbm.1, f32[16,64,1024]{2,1,0:T(8,128)} %w_gate.1, ...), custom_call_target="tpu_custom_call" | custom-call | tf_op jit(solution)/shard_map/exchange/pallas_call | solution.py:346
  58.5 2.2 %write_out.1 = (bf16[16,32,2048]{2,1,0:T(8,128)(2,1)}, bf16[16,32,2048]{2,1,0:T(8,128)(2,1)}, f32[16,32]{1,0:T(8,128)}, f32[16,32]{1,0:T(8,128)}, bf16[64,2048]{1,0:T(8,128)(2,1)}) custom-call(bf16[16,32,2048]{2,1,0:T(8,128)(2,1)S(1)} %get-tuple-element.16.gate, bf16[16,32,2048]{2,1,0:T(8,128)(2,1)S(1)} %get-tuple-element.17.up, ...), custom_call_target="tpu_custom_call" | custom-call | tf_op jit(solution)/shard_map/write_out/pallas_call | solution.py:391

commit v8 on v7

--- a/solution.py
+++ b/solution.py
@@ -16,7 +16,7 @@
 THIRD = 12
 LATE = 14
 OFFSETS = [(a, b, c) for a in range(4) for b in range(2) for c in range(4)][1:]
-FARTHEST = sorted(OFFSETS, key=lambda o: -min(o[0], 4 - o[0]) - 2 * o[1] - min(o[2], 4 - o[2]))
+FARTHEST = sorted(OFFSETS, key=lambda o: -min(o[0], 4 - o[0]) - 8 * o[1] - min(o[2], 4 - o[2]))
 
 
 def left_half(shape):

time: 60.8 us -> 61 us (level)
  no operation moved by 1% of the time
where the time goes in v8:
time: 61 us; the launch traced here: 60.9 us
  Pallas kernels  60.2 us (99%)
  between operations  0.64 us (1%)
    pallas_call x1, Pallas kernels, body(): pl.pallas_call(exchange, out_shape=[pltpu.VMEM(*shape) for shape in carri...  58.1 us
    pallas_call x1, Pallas kernels, body(): pl.pallas_call(write_out, out_shape=[jax.ShapeDtypeStruct(*shape) for sha...  2.15 us

profile of v8, /device:TPU:0, one launch (start us, length us, event | category | flops | bytes accessed | tf_op | source)
XLA Modules:
  0.0 60.9 jit_solution(7058141133680903101)
XLA Ops:
  0.6 58.1 %exchange.1 = (bf16[16,32,2048]{2,1,0:T(8,128)(2,1)S(1)}, bf16[16,32,2048]{2,1,0:T(8,128)(2,1)S(1)}, bf16[64,2048]{1,0:T(8,128)(2,1)S(1)}, f32[32,128]{1,0:T(8,1...) custom-call(f32[16]{0:T(128)} %mix_hbm.1, f32[16,64,1024]{2,1,0:T(8,128)} %w_gate.1, ...), custom_call_target="tpu_custom_call" | custom-call | tf_op jit(solution)/shard_map/exchange/pallas_call | solution.py:346
  58.7 2.2 %write_out.1 = (bf16[16,32,2048]{2,1,0:T(8,128)(2,1)}, bf16[16,32,2048]{2,1,0:T(8,128)(2,1)}, f32[16,32]{1,0:T(8,128)}, f32[16,32]{1,0:T(8,128)}, bf16[64,2048]{1,0:T(8,128)(2,1)}) custom-call(bf16[16,32,2048]{2,1,0:T(8,128)(2,1)S(1)} %get-tuple-element.16.gate, bf16[16,32,2048]{2,1,0:T(8,128)(2,1)S(1)} %get-tuple-element.17.up, ...), custom_call_target="tpu_custom_call" | custom-call | tf_op jit(solution)/shard_map/write_out/pallas_call | solution.py:391
